TPU v7x, 32 devices: a whole 2x2x4 slice. The times are simulated.
32 devices in a mesh: blk: 4 (over y, x), grp: 8 (over z, core).
Axes of the slice: x: 2, y: 2, z: 4, core: 2. Of those that a mesh axis runs over, the one named last changes fastest.
Arguments:
- b3c: bfloat16 [384, 3, 32, 4096], P('blk', None, None, 'grp'), may hold values from -6 to 6
- green_occ: bfloat16 [384, 384], P('blk', 'grp'), may hold values from -0.3125 to 0.3125
- green_virt: bfloat16 [384, 384], P(None, 'grp'), may hold values from -0.625 to 0.625
- occ_mask: int32 [12, 12], replicated, may hold values from 0 to 1, as said below
- a_tiles: bfloat16 [128, 32, 1024], P(('blk', 'grp')), may hold values from -0.046875 to 0.046875
- tile_codes: int32 [128], P(('blk', 'grp')), may hold values from -1 to 143, as said below
Outputs:
- chi: float32 [512, 4096], P('blk', 'grp')
Inputs may be any that keep to these rules, and one draw needn't show every extreme that they name: `occ_mask`: the diagonal is 1. `tile_codes`: each device's 4 slots hold its live tiles first and -1 after them; some device has all 4 slots live; codes may repeat, and repeated tiles add.
All inputs are finite; a program needn't handle non-finite values.
Results may differ from a plain program's by a relative error of at most 0.0041.
Values may be sent and summed in bfloat16 or wider, within the bound.
No kernel may reach another device: no remote copies, remote signals or barrier semaphores. Data moves between devices by JAX's collectives and lax.ppermute only.
A program may use at most 192 MiB of HBM per device.

v0:
```python
import jax
import jax.numpy as jnp
from jax import lax
from jax.sharding import PartitionSpec as P

BS = 32
PB = 32
KB = 3
BAND = 3
PBD = 4


def local(b3c, green_occ, green_virt, occ_mask, a_tiles, tile_codes):
    group = lax.axis_index("blk")
    occ_all, virt_all = (
        lax.all_gather(green_occ, "grp", axis=1, tiled=True),
        lax.all_gather(green_virt, "grp", axis=1, tiled=True),
    )
    basis_total = virt_all.shape[1]
    block_total = basis_total // BS
    window = (KB + BAND - 1) * BS
    pair_count = KB * BAND
    query_local = b3c.shape[3]
    mask_rows = lax.dynamic_slice_in_dim(occ_mask, group * KB, KB, 0)
    mask_full = jnp.repeat(jnp.repeat(mask_rows, BS, axis=0), BS, axis=1).astype(jnp.bfloat16)
    occ_group = occ_all * mask_full
    rows = (group * KB * BS + jnp.arange(window, dtype=jnp.int32)) % basis_total
    virt_window = jnp.take(virt_all, rows, axis=0).reshape(window, block_total, BS)
    accumulate_piece = lax.all_gather(b3c, "blk", axis=0, tiled=True)
    count = accumulate_piece.shape[0]
    blocks_in = count // BS
    lam_index = jnp.arange(count, dtype=jnp.int32) % basis_total
    occ_cols = jnp.take(occ_group, lam_index, axis=1)
    lam_blocks = jnp.arange(blocks_in, dtype=jnp.int32) % block_total
    partner = (lam_blocks[:, None] + jnp.arange(BAND, dtype=jnp.int32)[None, :]) % block_total
    virt_sel = jnp.take(virt_window, partner, axis=1)
    tensor = accumulate_piece.reshape(blocks_in, BS, BAND, BS, query_local)
    inner = jnp.einsum("wlds,ladsq->lawq", virt_sel, tensor, preferred_element_type=jnp.float32)
    inner = inner.astype(jnp.bfloat16).reshape(count, window * query_local)
    paired = jnp.dot(occ_cols, inner, preferred_element_type=jnp.float32)
    paired = paired.reshape(KB * BS, window, query_local).astype(jnp.bfloat16)
    pieces = []
    for block in range(KB):
        for offset in range(BAND):
            piece = paired[
                block * BS : (block + 1) * BS, (block + offset) * BS : (block + offset + 1) * BS
            ]
            pieces.append(piece.reshape(BS * BS, query_local))
    pairs = jnp.stack(pieces)
    aux_blocks = lax.axis_size("blk") * PBD
    tiles = lax.all_gather(a_tiles, "grp", axis=0, tiled=True)
    codes = lax.all_gather(tile_codes, "grp", axis=0, tiled=True)
    count = tiles.shape[0]
    valid = codes >= 0
    pair = jnp.where(valid, codes % pair_count, 0).astype(jnp.int32)
    pblock = jnp.where(valid, codes // pair_count, -1).astype(jnp.int32)
    chosen = jnp.take(pairs, pair, axis=0)
    contrib = jnp.einsum("tik,tkq->tiq", tiles, chosen, preferred_element_type=jnp.float32)
    selector = (jnp.arange(aux_blocks, dtype=jnp.int32)[:, None] == pblock[None, :]).astype(
        jnp.float32
    )
    partial_chi = jnp.dot(
        selector, contrib.reshape(count, PB * query_local), precision=lax.Precision.HIGHEST
    )
    partial_chi = partial_chi.reshape(aux_blocks * PB, query_local)
    return lax.psum_scatter(partial_chi, "blk", scatter_dimension=0, tiled=True)


def solution(mesh):
    in_specs = (
        P("blk", None, None, "grp"),
        P("blk", "grp"),
        P(None, "grp"),
        P(),
        P(("blk", "grp"), None, None),
        P(("blk", "grp")),
    )
    out_specs = P("blk", "grp")
    return jax.shard_map(local, mesh=mesh, in_specs=in_specs, out_specs=out_specs, check_vma=False)
```

profile of v0, /device:TPU:0, one launch (start us, length us, event | category | flops | bytes accessed | tf_op | source)
XLA Modules:
  0.0 637.7 jit_solution(16914202088193835434)
XLA Ops:
  6.5 0.0 copy-start.5
  6.5 0.0 copy-start.3
  6.5 0.0 copy-start.1
  6.5 0.0 copy-start
  6.5 0.0 all-gather.3.cloned.1.call-start
  6.6 0.7 all-gather.3.cloned.1.call-update
  7.3 0.0 all-gather.5.cloned.1.call-start
  7.3 0.7 all-gather.5.cloned.1.call-update
  8.0 0.0 reduce-scatter.2.cloned.1.call-start
  8.2 0.0 copy-done.5
  8.2 0.6 dynamic-slice
  9.4 0.0 copy-done.3
  9.4 0.2 dynamic-update-slice
  9.7 10.6 %all-reduce = s32[32]{0:T(128)S(1)} all-reduce(s32[32]{0:T(128)S(1)} %dynamic-update-slice), channel_id=1, replica_groups=mesh['blk'=4,'grp'=8] {'grp'}, use_global_device_ids=true, to_apply=%add | all-reduce | flops 32 | bytes 256
  20.3 0.5 compare_and_fusion.2
  20.9 0.5 compare_select_fusion.6
  21.4 0.7 dynamic-slice_convert_fusion
  22.1 0.1 copy.26
  22.2 0.1 broadcast_in_dim.57
  22.3 0.1 convert_element_type.22
  22.4 0.0 copy-done.1
  22.4 13.9 %all_gather.16 = bf16[96,384]{0,1:T(8,128)(2,1)S(1)} all-gather(bf16[96,48]{0,1:T(8,128)(2,1)S(1)} %copy-done.1), channel_id=1, replica_groups=mesh['blk'=4,'grp'=8] {'grp'}, dimensions={1}, use_global_device_ids=true | all-gather | bytes 82944 | tf_op jit(solution)/shard_map/all_gather | solution.py:16
  36.3 0.0 copy-done
  36.3 14.2 %all_gather.17 = bf16[384,384]{0,1:T(8,128)(2,1)S(1)} all-gather(bf16[384,48]{0,1:T(8,128)(2,1)S(1)} %copy-done), channel_id=1, replica_groups=mesh['blk'=4,'grp'=8] {'grp'}, dimensions={1}, use_global_device_ids=true | all-gather | bytes 331776 | tf_op jit(solution)/shard_map/all_gather | solution.py:17
  50.6 0.2 copy.27
  50.8 0.9 gather_fusion.1
  51.7 0.1 copy.28
  51.9 0.1 reshape.161
  52.0 0.6 pad_clamp_fusion
  52.6 1.4 gather_fusion
  54.1 0.6 gather_fusion.2
  54.7 290.2 %all-gather.3.cloned.1.call-done = bf16[384,3,32,512]{3,2,1,0:T(8,128)(2,1)} async-done(((bf16[96,3,32,512]{3,2,1,0:T(8,128)(2,1)}), bf16[384,3,32,512]{3,2,1,0:T(8,128)(2,1)}) %all-gather.3.cloned.1.call-update) | async-done | bytes 37748752 | tf_op jit(solution)/shard_map/all_gather | solution.py:29
  344.8 36.7 %bitcast_convert_fusion = bf16[12,160,32,512]{3,1,2,0:T(8,128)(2,1)} fusion(bf16[12,32,3,32,512]{4,3,2,1,0:T(8,128)(2,1)} %bitcast.86, bf16[12,3,160,32]{2,3,1,0:T(8,128)(2,1)S(1)} %bitcast.73, pred[12,3]{1,0:T(8,128)(4,1)S(1)} %compare_and_fusion), kind=kOutput, calls=%fused_computation.4 | convolution fusion | flops 6071439360 | bytes 101031968 | tf_op jit(solution)/shard_map/wlds,ladsq->lawq/dot_general | solution.py:38
  381.5 56.2 %copy.44 = bf16[48,8,160,512]{3,1,2,0:T(8,128)(2,1)} copy(bf16[48,8,160,512]{3,2,1,0:T(8,128)(2,1)} %bitcast.71) | data formatting | bytes 125829120
  437.7 80.5 %copy.29 = bf16[81920,384]{1,0:T(8,128)(2,1)} copy(bf16[81920,384]{0,1:T(8,128)(2,1)} %bitcast.70) | data formatting | bytes 125829120 | tf_op jit(solution)/shard_map/dot_general | solution.py:40
  518.2 31.3 %convolution_convert_fusion = bf16[96,160,512]{2,0,1:T(8,128)(2,1)} fusion(bf16[160,512,384]{2,1,0:T(8,128)(2,1)} %bitcast.69, bf16[384,96]{1,0:T(8,128)(2,1)S(1)} %gather_fusion, pred[384]{0:T(512)(128)(4,1)S(1)} %iota_compare_fusion.2), kind=kOutput, calls=%fused_computation.9 | convolution fusion | flops 6047698944 | bytes 78717312 | tf_op jit(solution)/shard_map/dot_general | solution.py:40
  549.5 4.3 fusion.23
  553.8 0.6 copy.31
  554.4 0.6 copy.32
  555.0 0.6 copy.33
  555.5 0.6 copy.34
  556.1 0.6 copy.35
  556.7 0.6 copy.36
  557.3 0.6 copy.37
  557.9 0.6 copy.38
  558.5 0.6 copy.39
  559.1 1.1 bitcast_dynamic-update-slice_fusion.8
  560.1 1.1 bitcast_dynamic-update-slice_fusion.7
  561.2 1.0 bitcast_dynamic-update-slice_fusion.6
  562.2 1.1 bitcast_dynamic-update-slice_fusion.5
  563.3 1.0 bitcast_dynamic-update-slice_fusion.4
  564.4 1.0 bitcast_dynamic-update-slice_fusion.3
  565.4 1.1 bitcast_dynamic-update-slice_fusion.2
  566.5 1.1 bitcast_dynamic-update-slice_fusion.1
  567.5 1.0 bitcast_dynamic-update-slice_fusion
  568.6 16.6 %gather_fusion.3 = bf16[32,1024,512]{2,1,0:T(8,128)(2,1)} fusion(bf16[9,1024,512]{2,1,0:T(8,128)(2,1)} %bitcast_dynamic-update-slice_fusion, s32[1024]{0:T(1024)} %pad_clamp_fusion), kind=kCustom, calls=%fused_computation.3 | custom fusion | bytes 67108992 | tf_op jit(solution)/shard_map/jit(_take)/gather | solution.py:57
  585.2 0.0 copy-done.4
  585.2 14.7 %fusion = f32[32,512,32]{1,2,0:T(8,128)S(1)} fusion(bf16[32,32,1024]{2,1,0:T(8,128)(2,1)} %all-gather.5.cloned.1.call-done, bf16[32,1024,512]{2,1,0:T(8,128)(2,1)} %gather_fusion.3, pred[32]{0:T(512)(128)(4,1)S(1)} %copy-done.4), kind=kOutput, calls=%fused_computation.5 | convolution fusion | flops 1090519040 | bytes 37748768 | tf_op jit(solution)/shard_map/tik,tkq->tiq/dot_general | solution.py:58
  599.9 1.2 copy.45
  601.1 0.0 copy-done.2
  601.1 0.8 fusion.18
  601.9 1.2 reshape.142
  603.1 0.0 reduce-scatter.2.cloned.1.call-update
  603.1 28.1 %reduce-scatter.2.cloned.1.call-done = f32[128,512]{1,0:T(8,128)} async-done(((f32[512,512]{1,0:T(8,128)}), f32[128,512]{1,0:T(8,128)}) %reduce-scatter.2.cloned.1.call-update) | async-done | bytes 262160 | tf_op jit(solution)/shard_map/reduce_scatter | solution.py:66
  (15 shorter events, 0.1 us)
Async XLA Ops:
  6.5 1.6 copy-start.5
  6.5 2.9 copy-start.3
  6.5 15.9 %copy-start.1 = (bf16[96,48]{0,1:T(8,128)(2,1)S(1)}, bf16[96,48]{0,1:T(8,128)(2,1)}, u32[]{:S(2)}) copy-start(bf16[96,48]{0,1:T(8,128)(2,1)} %param.7) | copy-start | bytes 27652
  6.5 29.8 %copy-start = (bf16[384,48]{0,1:T(8,128)(2,1)S(1)}, bf16[384,48]{0,1:T(8,128)(2,1)}, u32[]{:S(2)}) copy-start(bf16[384,48]{0,1:T(8,128)(2,1)} %param.8) | copy-start | bytes 110596
  6.5 338.3 %all-gather.3.cloned.1.call-start = ((), (), s32[]{:S(2)}) async-start(), calls=%async_computation.1 | async-start | bytes 47185920 | tf_op jit(solution)/shard_map/all_gather | solution.py:29
  7.3 577.9 %all-gather.5.cloned.1.call-start = ((), (), s32[]{:S(2)}) async-start(), calls=%async_computation.2 | async-start | bytes 2359296 | tf_op jit(solution)/shard_map/all_gather | solution.py:51
  8.0 623.2 %reduce-scatter.2.cloned.1.call-start = ((), (), s32[]{:S(2)}) async-start(), calls=%async_computation.3 | async-start | bytes 1310720 | tf_op jit(solution)/shard_map/reduce_scatter | solution.py:66
  568.6 16.6 %copy-start.4 = (pred[32]{0:T(512)(128)(4,1)S(1)}, pred[32]{0:T(512)(128)(4,1)}, u32[]{:S(2)}) copy-start(pred[32]{0:T(512)(128)(4,1)} %get-tuple-element.5) | copy-start | bytes 100
  585.2 15.9 %copy-start.2 = (s32[32]{0:T(128)S(1)}, s32[32]{0:T(128)}, u32[]{:S(2)}) copy-start(s32[32]{0:T(128)} %compare_select_fusion.6) | copy-start | bytes 388
Sparse Core Ops, SparseCore 0:
  9.2 335.5 all-gather.2
  346.4 29.1 all-gather.4
  603.2 27.9 reduce-scatter.1
where the time goes:
time: 640 us; the launch traced here: 638 us
  waiting for transfers between devices  320 us (50%)
  local copies, waits for them, and re-layouts  179 us (28%)
  matrix products  83.5 us (13%)
  blocking collectives  38.8 us (6%)
  between operations  14 us (2%)
    all_gather x1, waiting for transfers between devices, local(): accumulate_piece = lax.all_gather(b3c, 'blk', axis=0, tiled=True)  290 us
    dot_general x1, local copies, waits for them, and re-layouts, local(): paired = jnp.dot(occ_cols, inner, preferred_element_type=jnp.float32)  80.5 us
    unnamed x25, local copies, waits for them, and re-layouts  66.7 us
    dot_general x1, matrix products, local(): jnp.einsum('wlds,ladsq->lawq', virt_sel, tensor, preferred_element_type=j...  36.7 us
    dot_general x1, matrix products, local(): paired = jnp.dot(occ_cols, inner, preferred_element_type=jnp.float32)  31.3 us
    reduce_scatter x1, waiting for transfers between devices, local(): return lax.psum_scatter(partial_chi, 'blk', scatter_dimension=0, tiled=True)  28.1 us
    gather x1, local copies, waits for them, and re-layouts, local(): chosen = jnp.take(pairs, pair, axis=0)  16.6 us
    dot_general x1, matrix products, local(): jnp.einsum('tik,tkq->tiq', tiles, chosen, preferred_element_type=jnp.floa...  14.7 us
  transfers between devices with their start and end apart: 3, of which 2 were waited for; matrix products, arithmetic and copies ran while one was open for 39% of the time, Pallas kernels for 0%

commit v1 on v0

--- a/solution.py
+++ b/solution.py
@@ -26,7 +26,12 @@
     occ_group = occ_all * mask_full
     rows = (group * KB * BS + jnp.arange(window, dtype=jnp.int32)) % basis_total
     virt_window = jnp.take(virt_all, rows, axis=0).reshape(window, block_total, BS)
-    accumulate_piece = lax.all_gather(b3c, "blk", axis=0, tiled=True)
+    ring = [b3c]
+    for hop in range(3):
+        ring.append(lax.ppermute(ring[-1], "blk", [(dev, (dev + 1) % 4) for dev in range(4)]))
+    accumulate_piece = jnp.roll(
+        jnp.concatenate(ring[::-1], axis=0), (lax.axis_index("blk") + 1) * ring[0].shape[0], axis=0
+    )
     count = accumulate_piece.shape[0]
     blocks_in = count // BS
     lam_index = jnp.arange(count, dtype=jnp.int32) % basis_total

time: 640 us -> 1010 us (1.58)
  waiting for transfers between devices: 320 us -> 592 us
  local copies, waits for them, and re-layouts: 179 us -> 277 us
    ppermute x0 -> x3, waiting for transfers between devices: none -> 564 us  [local(): lax.ppermute(ring[-1], 'blk', [(dev, (dev + 1) % 4) for dev in range(4)])]
    all_gather x1 -> x0, waiting for transfers between devices: 290 us -> none  [local(): accumulate_piece = lax.all_gather(b3c, 'blk', axis=0, tiled=True)]
    unnamed x25 -> x30, local copies, waits for them, and re-layouts: 66.7 us -> 136 us
    dynamic_slice x0 -> x1, local copies, waits for them, and re-layouts: none -> 25.4 us  [local(): jnp.roll(jnp.concatenate(ring[::-1], axis=0), (lax.axis_index('blk') + 1)...]
  transfers between devices with their start and end apart: 3 -> 5, of which waited for: 2 -> 4; matrix products, arithmetic and copies ran while one was open for 39% -> 34% of each run, Pallas kernels for 0% -> 0%
where the time goes in v1:
time: 1010 us
  waiting for transfers between devices  592 us (59%)
  local copies, waits for them, and re-layouts  277 us (27%)
  matrix products  83.4 us (8%)
  blocking collectives  39.2 us (4%)
  between operations  14.2 us (1%)
    ppermute x3, waiting for transfers between devices, local(): lax.ppermute(ring[-1], 'blk', [(dev, (dev + 1) % 4) for dev in range(4)])  564 us
    unnamed x30, local copies, waits for them, and re-layouts  136 us
    dot_general x1, local copies, waits for them, and re-layouts, local(): paired = jnp.dot(occ_cols, inner, preferred_element_type=jnp.float32)  73.1 us
    dot_general x1, matrix products, local(): jnp.einsum('wlds,ladsq->lawq', virt_sel, tensor, preferred_element_type=j...  36.5 us
    dot_general x1, matrix products, local(): paired = jnp.dot(occ_cols, inner, preferred_element_type=jnp.float32)  31.3 us
    reduce_scatter x1, waiting for transfers between devices, local(): return lax.psum_scatter(partial_chi, 'blk', scatter_dimension=0, tiled=True)  27.9 us
    dynamic_slice x1, local copies, waits for them, and re-layouts, local(): jnp.roll(jnp.concatenate(ring[::-1], axis=0), (lax.axis_index('blk') + 1)...  25.4 us
  transfers between devices with their start and end apart: 5, of which 4 were waited for; matrix products, arithmetic and copies ran while one was open for 34% of the time, Pallas kernels for 0%

profile of v1, /device:TPU:0, one launch (start us, length us, event | category | flops | bytes accessed | tf_op | source)
XLA Modules:
  0.0 1011.6 jit_solution(1579673558141053420)
XLA Ops:
  6.5 3.0 collective-permute-start
  9.5 204.1 %collective-permute-done = bf16[96,3,32,512]{3,2,1,0:T(8,128)(2,1)S(1)} collective-permute-done((bf16[96,3,32,512]{3,2,1,0:T(8,128)(2,1)}, bf16[96,3,32,512]{3,2,1,0:T(8,128)(2,1)S(1)}, u32[]{:S(2)}, u32[]{:S(2)}) %collective-permute-start) | collective-permute-done | bytes 9437216 | tf_op jit(solution)/shard_map/ppermute | solution.py:31
  213.6 3.7 copy-done
  217.3 0.8 collective-permute-start.1
  218.0 204.3 %collective-permute-done.1 = bf16[96,3,32,512]{3,2,1,0:T(8,128)(2,1)} collective-permute-done((bf16[96,3,32,512]{3,2,1,0:T(8,128)(2,1)S(1)}, bf16[96,3,32,512]{3,2,1,0:T(8,128)(2,1)}, u32[]{:S(2)}, u32[]{:S(2)}) %collective-permute-start.1) | collective-permute-done | bytes 9437216 | tf_op jit(solution)/shard_map/ppermute | solution.py:31
  422.4 0.0 reduce-scatter.2.cloned.1.call-start
  422.5 14.6 %all_gather.14 = bf16[384,384]{0,1:T(8,128)(2,1)S(1)} all-gather(bf16[384,48]{0,1:T(8,128)(2,1)} %param.8), channel_id=1, replica_groups=mesh['blk'=4,'grp'=8] {'grp'}, dimensions={1}, use_global_device_ids=true | all-gather | bytes 331776 | tf_op jit(solution)/shard_map/all_gather | solution.py:17
  437.1 0.2 copy.27
  437.4 0.9 gather_fusion.1
  438.3 0.1 copy.28
  438.5 0.1 reshape.161
  438.6 0.7 dynamic-slice_convert_fusion
  439.3 0.1 copy.26
  439.4 0.1 broadcast_in_dim.57
  439.5 0.1 convert_element_type.22
  439.6 0.6 gather_fusion.2
  440.2 15.5 %all_gather.13 = bf16[96,384]{0,1:T(8,128)(2,1)S(1)} all-gather(bf16[96,48]{0,1:T(8,128)(2,1)} %param.7), channel_id=1, replica_groups=mesh['blk'=4,'grp'=8] {'grp'}, dimensions={1}, use_global_device_ids=true | all-gather | bytes 82944 | tf_op jit(solution)/shard_map/all_gather | solution.py:16
  455.7 1.9 gather_fusion
  457.6 1.2 dynamic-slice
  459.4 0.9 dynamic-update-slice
  460.3 9.0 all-reduce
  469.3 0.6 iota_compare_fusion.2
  469.9 0.5 compare_and_fusion.2
  470.4 0.6 pad_clamp_fusion
  471.0 0.5 compare_select_fusion.6
  471.6 155.2 %collective-permute-done.2 = bf16[96,3,32,512]{3,2,1,0:T(8,128)(2,1)} collective-permute-done((bf16[96,3,32,512]{3,2,1,0:T(8,128)(2,1)}, bf16[96,3,32,512]{3,2,1,0:T(8,128)(2,1)}, u32[]{:S(2)}, u32[]{:S(2)}) %collective-permute-start.2) | collective-permute-done | bytes 9437216 | tf_op jit(solution)/shard_map/ppermute | solution.py:31
  626.8 9.3 constant_dynamic-update-slice_fusion.7
  636.1 9.3 constant_dynamic-update-slice_fusion.6
  645.3 9.3 constant_dynamic-update-slice_fusion.5
  654.7 9.3 constant_dynamic-update-slice_fusion.4
  663.9 9.2 constant_dynamic-update-slice_fusion.3
  673.1 9.2 constant_dynamic-update-slice_fusion.2
  682.3 9.2 constant_dynamic-update-slice_fusion.1
  691.5 9.1 constant_dynamic-update-slice_fusion
  700.6 25.4 %constant_dynamic-slice_fusion = bf16[384,3,32,512]{3,2,1,0:T(8,128)(2,1)} fusion(bf16[768,3,32,512]{3,2,1,0:T(8,128)(2,1)} %constant_dynamic-update-slice_fusion, s32[]{:T(128)S(6)} %select_n.147), kind=kLoop, calls=%fused_computation.70 | loop fusion | bytes 75497472 | tf_op jit(solution)/shard_map/jit(_roll_dynamic)/dynamic_slice | solution.py:32
  726.0 36.5 %bitcast_convert_fusion = bf16[12,32,512,160]{2,3,1,0:T(8,128)(2,1)} fusion(bf16[12,32,3,32,512]{4,3,2,1,0:T(8,128)(2,1)} %bitcast.72, bf16[12,3,160,32]{2,3,1,0:T(8,128)(2,1)S(1)} %bitcast.73, pred[12,3]{1,0:T(8,128)(4,1)S(1)} %compare_and_fusion), kind=kOutput, calls=%fused_computation.4 | convolution fusion | flops 6071439360 | bytes 101031968 | tf_op jit(solution)/shard_map/wlds,ladsq->lawq/dot_general | solution.py:43
  762.6 56.2 %copy.44 = bf16[48,8,160,512]{3,1,2,0:T(8,128)(2,1)} copy(bf16[48,8,160,512]{3,2,1,0:T(8,128)(2,1)} %bitcast.70) | data formatting | bytes 125829120
  818.8 73.1 %copy.29 = bf16[81920,384]{1,0:T(8,128)(2,1)} copy(bf16[81920,384]{0,1:T(8,128)(2,1)} %bitcast.71) | data formatting | bytes 125829120 | tf_op jit(solution)/shard_map/dot_general | solution.py:45
  891.9 31.3 %convolution_convert_fusion = bf16[96,160,512]{2,0,1:T(8,128)(2,1)} fusion(bf16[160,512,384]{2,1,0:T(8,128)(2,1)} %bitcast.69, bf16[384,96]{1,0:T(8,128)(2,1)S(1)} %copy-done.1, pred[384]{0:T(512)(128)(4,1)S(1)} %copy-done.3), kind=kOutput, calls=%fused_computation.9 | convolution fusion | flops 6047698944 | bytes 78717312 | tf_op jit(solution)/shard_map/dot_general | solution.py:45
  923.2 4.4 fusion.23
  927.5 0.6 copy.31
  928.1 0.6 copy.32
  928.7 0.6 copy.33
  929.3 0.6 copy.34
  929.9 0.6 copy.35
  930.5 0.6 copy.36
  931.1 0.6 copy.37
  931.6 0.6 copy.38
  932.2 0.6 copy.39
  932.8 1.1 bitcast_dynamic-update-slice_fusion.8
  933.9 1.1 bitcast_dynamic-update-slice_fusion.7
  935.0 1.0 bitcast_dynamic-update-slice_fusion.6
  936.0 1.1 bitcast_dynamic-update-slice_fusion.5
  937.1 1.0 bitcast_dynamic-update-slice_fusion.4
  938.2 1.0 bitcast_dynamic-update-slice_fusion.3
  939.2 1.1 bitcast_dynamic-update-slice_fusion.2
  940.3 1.1 bitcast_dynamic-update-slice_fusion.1
  941.3 1.0 bitcast_dynamic-update-slice_fusion
  942.4 16.6 %gather_fusion.3 = bf16[32,1024,512]{2,1,0:T(8,128)(2,1)} fusion(bf16[9,1024,512]{2,1,0:T(8,128)(2,1)} %bitcast_dynamic-update-slice_fusion, s32[1024]{0:T(1024)} %pad_clamp_fusion), kind=kCustom, calls=%fused_computation.3 | custom fusion | bytes 67108992 | tf_op jit(solution)/shard_map/jit(_take)/gather | solution.py:62
  959.0 14.7 %fusion = f32[32,512,32]{1,2,0:T(8,128)S(1)} fusion(bf16[32,32,1024]{2,1,0:T(8,128)(2,1)} %all-gather.2.cloned.1.call-done, bf16[32,1024,512]{2,1,0:T(8,128)(2,1)} %gather_fusion.3, pred[32]{0:T(512)(128)(4,1)S(1)} %copy-done.4), kind=kOutput, calls=%fused_computation.5 | convolution fusion | flops 1090519040 | bytes 37748768 | tf_op jit(solution)/shard_map/tik,tkq->tiq/dot_general | solution.py:63
  973.7 1.2 copy.45
  974.9 0.8 fusion.18
  975.8 1.2 reshape.142
  976.9 27.9 %reduce-scatter.2.cloned.1.call-done = f32[128,512]{1,0:T(8,128)} async-done(((f32[512,512]{1,0:T(8,128)}), f32[128,512]{1,0:T(8,128)}) %reduce-scatter.2.cloned.1.call-update) | async-done | bytes 262160 | tf_op jit(solution)/shard_map/reduce_scatter | solution.py:71
  (25 shorter events, 0.2 us)
Async XLA Ops:
  6.5 952.4 %all-gather.2.cloned.1.call-start = ((), (), s32[]{:S(2)}) async-start(), calls=%async_computation.1 | async-start | bytes 2359296 | tf_op jit(solution)/shard_map/all_gather | solution.py:56
  6.5 207.1 %collective-permute-start = (bf16[96,3,32,512]{3,2,1,0:T(8,128)(2,1)}, bf16[96,3,32,512]{3,2,1,0:T(8,128)(2,1)S(1)}, u32[]{:S(2)}, u32[]{:S(2)}) collective-permute-start(bf16[96,3,32,512]{3,2,1,0:T(8,128)(2,1)} %param.6), channel_id=1, source_target_pairs={{0,8},{8,16},{16,24},{24,0},{1,9},{9,17},{17,25},{25,1},{2,10},{10... | collective-permute-start | bytes 28311560 | tf_op jit(solution)/shard_map/ppermute | solution.py:31
  213.6 3.7 copy-start
  217.3 205.1 %collective-permute-start.1 = (bf16[96,3,32,512]{3,2,1,0:T(8,128)(2,1)S(1)}, bf16[96,3,32,512]{3,2,1,0:T(8,128)(2,1)}, u32[]{:S(2)}, u32[]{:S(2)}) collective-permute-start(bf16[96,3,32,512]{3,2,1,0:T(8,128)(2,1)S(1)} %collective-permute-done), channel_id=1, source_target_pairs={{0,8},{8,16},{16,24},{24,0},{1,9},{9,17},{17,25},{25,1},{2,10},{10... | collective-permute-start | bytes 28311560 | tf_op jit(solution)/shard_map/ppermute | solution.py:31
  422.4 204.4 %collective-permute-start.2 = (bf16[96,3,32,512]{3,2,1,0:T(8,128)(2,1)}, bf16[96,3,32,512]{3,2,1,0:T(8,128)(2,1)}, u32[]{:S(2)}, u32[]{:S(2)}) collective-permute-start(bf16[96,3,32,512]{3,2,1,0:T(8,128)(2,1)} %collective-permute-done.1), channel_id=1, source_target_pairs={{0,8},{8,16},{16,24},{24,0},{1,9},{9,17},{17,25},{25,1},{2,10},{10... | collective-permute-start | bytes 28311560 | tf_op jit(solution)/shard_map/ppermute | solution.py:31
  422.4 582.4 %reduce-scatter.2.cloned.1.call-start = ((), (), s32[]{:S(2)}) async-start(), calls=%async_computation.2 | async-start | bytes 1310720 | tf_op jit(solution)/shard_map/reduce_scatter | solution.py:71
  818.8 73.1 %copy-start.1 = (bf16[384,96]{1,0:T(8,128)(2,1)S(1)}, bf16[384,96]{1,0:T(8,128)(2,1)}, u32[]{:S(2)}) copy-start(bf16[384,96]{1,0:T(8,128)(2,1)} %gather_fusion) | copy-start | bytes 221188
  818.8 73.1 %copy-start.3 = (pred[384]{0:T(512)(128)(4,1)S(1)}, pred[384]{0:T(512)(128)(4,1)}, u32[]{:S(2)}) copy-start(pred[384]{0:T(512)(128)(4,1)} %iota_compare_fusion.2) | copy-start | bytes 1156
  942.4 16.6 %copy-start.4 = (pred[32]{0:T(512)(128)(4,1)S(1)}, pred[32]{0:T(512)(128)(4,1)}, u32[]{:S(2)}) copy-start(pred[32]{0:T(512)(128)(4,1)} %get-tuple-element.5) | copy-start | bytes 100
  959.0 15.9 %copy-start.2 = (s32[32]{0:T(128)S(1)}, s32[32]{0:T(128)}, u32[]{:S(2)}) copy-start(s32[32]{0:T(128)} %compare_select_fusion.6) | copy-start | bytes 388
Sparse Core Ops, SparseCore 0:
  422.5 32.3 all-gather.1
  977.1 27.6 reduce-scatter.1
